TPU v7x, 32 devices: a whole 2x2x4 slice. The times are simulated.
32 devices in a mesh: row: 4 (over z), col: 8 (over y, x, core).
Axes of the slice: x: 2, y: 2, z: 4, core: 2. Of those that a mesh axis runs over, the one named last changes fastest.
Arguments:
- features: bfloat16 [32768, 256], P(('row', 'col')), may hold values from -6 to 6
- tile_values: bfloat16 [4, 8, 256, 128, 128], P('row', 'col'), may hold values from -0.09375 to 0.09375
- tile_rows: int32 [4, 8, 256], P('row', 'col'), may hold values from 0 to 63, as said below
- tile_cols: int32 [4, 8, 256], P('row', 'col'), may hold values from 0 to 31, as said below
- tile_count: int32 [4, 8], P('row', 'col'), may hold values from 64 to 256, as said below
- w_first: bfloat16 [256, 256], replicated, may hold values from -0.375 to 0.375
- w_second: bfloat16 [256, 256], replicated, may hold values from -0.375 to 0.375
Outputs:
- output: bfloat16 [32768, 256], P(('row', 'col'))
Inputs may be any that keep to these rules, and one draw needn't show every extreme that they name: `tile_rows`: in each block the slots name distinct tiles; the first tile_count slots are ordered by tile column, then tile row; later slots are padding. `tile_cols`: as for tile_rows. `tile_count`: some block uses all 256 slots.
All inputs are finite; a program needn't handle non-finite values.
Results may differ from a plain program's by a relative error of at most 0.024.
Values may be sent and summed in bfloat16 or wider, within the bound.
A program may use at most 192 MiB of HBM per device.

v0:
```python
import jax
import jax.numpy as jnp
from jax import lax
from jax.sharding import PartitionSpec as P

GROUP = 64


def order_by(primary, secondary, stride, occupied, beyond):
    slot_ids = jnp.arange(primary.shape[0], dtype=jnp.int32)
    marked = jnp.where(occupied, primary * stride + secondary, beyond + slot_ids)
    slot_order = jnp.argsort(marked, stable=True)
    return (slot_order, marked[slot_order])


def accumulate(
    running, layout, slot_order, order_keys, key_low, key_high, panel_tiles, col_base, row_base
):
    values, row_ids, col_ids = layout
    group_size = GROUP
    first_pos = jnp.sum(order_keys < key_low)
    last_pos = jnp.sum(order_keys < key_high)
    group_low = first_pos // group_size
    group_high = (last_pos + group_size - 1) // group_size
    out_tiles = running.shape[0]
    tile_size = running.shape[1]
    feature_width = running.shape[2]
    out_ids = jnp.arange(out_tiles, dtype=jnp.int32)

    def group_step(group_index, current):
        positions = group_index * group_size + jnp.arange(group_size, dtype=jnp.int32)
        slot_ids = slot_order[positions]
        active = (positions >= first_pos) & (positions < last_pos)
        source = jnp.clip(col_ids[slot_ids] - col_base, 0, panel_tiles.shape[0] - 1)
        target = row_ids[slot_ids] - row_base
        products = jnp.einsum(
            "gij,gjf->gif",
            values[slot_ids],
            panel_tiles[source],
            preferred_element_type=jnp.float32,
        )
        flat = products.reshape(group_size, tile_size * feature_width)
        high = flat.astype(jnp.bfloat16)
        low = (flat - high.astype(jnp.float32)).astype(jnp.bfloat16)
        selector = ((out_ids[:, None] == target[None, :]) & active[None, :]).astype(jnp.bfloat16)
        placed = jnp.dot(selector, high, preferred_element_type=jnp.float32)
        placed = placed + jnp.dot(selector, low, preferred_element_type=jnp.float32)
        return current + placed.reshape(out_tiles, tile_size, feature_width)

    return lax.fori_loop(group_low, group_high, group_step, running)


def propagate(inputs_now, weight, layout, by_column, row_tiles, col_tiles):
    node_dev, feature_width = inputs_now.shape
    tile_size = layout[0].shape[-1]
    zeroes = jnp.zeros((row_tiles, tile_size, feature_width), jnp.float32)
    panel_tiles = lax.all_gather(inputs_now, "row", axis=0, tiled=True).reshape(
        -1, tile_size, feature_width
    )
    partial_value = accumulate(
        zeroes, layout, by_column[0], by_column[1], 0, row_tiles * col_tiles, panel_tiles, 0, 0
    )
    rounded = partial_value.reshape(-1, feature_width).astype(jnp.bfloat16)
    summed = lax.psum_scatter(rounded, "col", scatter_dimension=0, tiled=True).astype(jnp.float32)
    aggregated = summed.astype(jnp.bfloat16)
    return jax.nn.relu(jnp.dot(aggregated, weight, preferred_element_type=jnp.float32)).astype(
        jnp.bfloat16
    )


def shards(features, tile_values, tile_rows, tile_cols, tile_count, w_first, w_second):
    tile_size = tile_values.shape[-1]
    values = tile_values[0, 0]
    row_ids = tile_rows[0, 0]
    col_ids = tile_cols[0, 0]
    filled = tile_count[0, 0]
    node_dev = features.shape[0]
    row_tiles = node_dev * lax.axis_size("col") // tile_size
    col_tiles = node_dev * lax.axis_size("row") // tile_size
    occupied = jnp.arange(values.shape[0], dtype=jnp.int32) < filled
    beyond = row_tiles * col_tiles
    by_column = order_by(col_ids, row_ids, row_tiles, occupied, beyond)
    layout = (values, row_ids, col_ids)
    hidden = propagate(features, w_first, layout, by_column, row_tiles, col_tiles)
    return propagate(hidden, w_second, layout, by_column, row_tiles, col_tiles)


def solution(mesh):
    return jax.shard_map(
        shards,
        mesh=mesh,
        in_specs=(
            P(("row", "col"), None),
            P("row", "col", None, None, None),
            P("row", "col", None),
            P("row", "col", None),
            P("row", "col"),
            P(),
            P(),
        ),
        out_specs=P(("row", "col"), None),
        check_vma=False,
    )
```

profile of v0, /device:TPU:0, one launch (start us, length us, event | category | flops | bytes accessed | tf_op | source)
XLA Modules:
  0.0 606.8 jit_solution(16120350971540093675)
XLA Ops:
  17.3 40.1 %all-gather.3.cloned.1.call-done = bf16[4096,256]{1,0:T(8,128)(2,1)} async-done(((bf16[1024,256]{1,0:T(8,128)(2,1)}), bf16[4096,256]{1,0:T(8,128)(2,1)}) %all-gather.3.cloned.1.call-update) | async-done | bytes 2097168 | tf_op jit(solution)/shard_map/all_gather | solution.py:57
  61.6 139.5 %while.22 = (s32[]{:T(128)}, f32[64,128,256]{2,1,0:T(8,128)}, s32[]{:T(128)}, s32[256]{0:T(256)S(1)}, s32[256]{0:T(256)S(1)}, /*index=5*/s32[]{:T(128)}, s32[]{:...) while((s32[]{:T(128)}, f32[64,128,256]{2,1,0:T(8,128)}, ...), condition=%wide.region_4.5_spmd.clone, body=%wide.region_3.4_spmd.clone.sunk | while | flops 1088442368 | bytes 127944272 | solution.py:50
  77.3 4.7 copy.16
  86.5 4.7 convolution_add_fusion.4
  91.3 5.7 copy.17
  97.0 11.1 %bitcast_add_fusion.4 = f32[64,128,256]{2,1,0:T(8,128)} fusion(f32[64,128,256]{2,1,0:T(8,128)} %get-tuple-element.350, f32[8,8,128,256]{3,2,1,0:T(8,128)} %copy.17), kind=kLoop, calls=%fused_computation.14.clone.1 | loop fusion | flops 2097152 | bytes 25165824 | tf_op jit(solution)/shard_map/while/body/add | solution.py:48
  123.8 4.7 copy.16
  133.0 4.7 convolution_add_fusion.4
  137.8 5.7 copy.17
  143.5 11.1 %bitcast_add_fusion.4 = f32[64,128,256]{2,1,0:T(8,128)} fusion(f32[64,128,256]{2,1,0:T(8,128)} %get-tuple-element.350, f32[8,8,128,256]{3,2,1,0:T(8,128)} %copy.17), kind=kLoop, calls=%fused_computation.14.clone.1 | loop fusion | flops 2097152 | bytes 25165824 | tf_op jit(solution)/shard_map/while/body/add | solution.py:48
  170.3 4.7 copy.16
  179.5 4.7 convolution_add_fusion.4
  184.3 5.7 copy.17
  190.0 11.1 %bitcast_add_fusion.4 = f32[64,128,256]{2,1,0:T(8,128)} fusion(f32[64,128,256]{2,1,0:T(8,128)} %get-tuple-element.350, f32[8,8,128,256]{3,2,1,0:T(8,128)} %copy.17), kind=kLoop, calls=%fused_computation.14.clone.1 | loop fusion | flops 2097152 | bytes 25165824 | tf_op jit(solution)/shard_map/while/body/add | solution.py:48
  201.1 5.9 convert_element_type.52
  207.1 96.6 %reduce-scatter.3.cloned.1.call-done = bf16[1024,256]{1,0:T(8,128)(2,1)} async-done(((bf16[8192,256]{1,0:T(8,128)(2,1)}), bf16[1024,256]{1,0:T(8,128)(2,1)}) %reduce-scatter.3.cloned.1.call-update) | async-done | bytes 524304 | tf_op jit(solution)/shard_map/reduce_scatter | solution.py:64
  305.9 45.7 %all-gather.5.cloned.1.call-done = bf16[4096,256]{1,0:T(8,128)(2,1)} async-done(((bf16[1024,256]{1,0:T(8,128)(2,1)}), bf16[4096,256]{1,0:T(8,128)(2,1)}) %all-gather.5.cloned.1.call-update) | async-done | bytes 2097168 | tf_op jit(solution)/shard_map/all_gather | solution.py:57
  355.9 139.6 %while.23 = (s32[]{:T(128)}, f32[64,128,256]{2,1,0:T(8,128)}, s32[]{:T(128)}, s32[256]{0:T(256)S(1)}, s32[256]{0:T(256)S(1)}, /*index=5*/s32[]{:T(128)}, s32[]{:...) while((s32[]{:T(128)}, f32[64,128,256]{2,1,0:T(8,128)}, ...), condition=%wide.region_7.8_spmd.clone, body=%wide.region_6.7_spmd.clone.sunk | while | flops 1088442368 | bytes 127944272 | solution.py:50
  371.6 4.7 copy.18
  380.8 4.7 convolution_add_fusion.5
  385.6 5.7 copy.19
  391.3 11.1 %bitcast_add_fusion.5 = f32[64,128,256]{2,1,0:T(8,128)} fusion(f32[64,128,256]{2,1,0:T(8,128)} %get-tuple-element.386, f32[8,8,128,256]{3,2,1,0:T(8,128)} %copy.19), kind=kLoop, calls=%fused_computation.36.clone.1 | loop fusion | flops 2097152 | bytes 25165824 | tf_op jit(solution)/shard_map/while/body/add | solution.py:48
  418.2 4.7 copy.18
  427.4 4.7 convolution_add_fusion.5
  432.1 5.7 copy.19
  437.8 11.1 %bitcast_add_fusion.5 = f32[64,128,256]{2,1,0:T(8,128)} fusion(f32[64,128,256]{2,1,0:T(8,128)} %get-tuple-element.386, f32[8,8,128,256]{3,2,1,0:T(8,128)} %copy.19), kind=kLoop, calls=%fused_computation.36.clone.1 | loop fusion | flops 2097152 | bytes 25165824 | tf_op jit(solution)/shard_map/while/body/add | solution.py:48
  464.7 4.7 copy.18
  473.9 4.7 convolution_add_fusion.5
  478.6 5.7 copy.19
  484.3 11.1 %bitcast_add_fusion.5 = f32[64,128,256]{2,1,0:T(8,128)} fusion(f32[64,128,256]{2,1,0:T(8,128)} %get-tuple-element.386, f32[8,8,128,256]{3,2,1,0:T(8,128)} %copy.19), kind=kLoop, calls=%fused_computation.36.clone.1 | loop fusion | flops 2097152 | bytes 25165824 | tf_op jit(solution)/shard_map/while/body/add | solution.py:48
  495.5 6.0 convert_element_type.55
  501.5 96.7 %reduce-scatter.5.cloned.1.call-done = bf16[1024,256]{1,0:T(8,128)(2,1)} async-done(((bf16[8192,256]{1,0:T(8,128)(2,1)}), bf16[1024,256]{1,0:T(8,128)(2,1)}) %reduce-scatter.5.cloned.1.call-update) | async-done | bytes 524304 | tf_op jit(solution)/shard_map/reduce_scatter | solution.py:64
  (113 shorter events, 141.1 us)
Async XLA Ops:
  6.5 297.1 %copy-start = (bf16[256,256]{1,0:T(8,128)(2,1)S(1)}, bf16[256,256]{1,0:T(8,128)(2,1)}, u32[]{:S(2)}) copy-start(bf16[256,256]{1,0:T(8,128)(2,1)} %param.16) | copy-start | bytes 393220
  6.5 55.0 %copy-start.3 = (s32[1,1,256]{2,1,0:T(1,128)S(1)}, s32[1,1,256]{2,1,0:T(1,128)}, u32[]{:S(2)}) copy-start(s32[1,1,256]{2,1,0:T(1,128)} %param.14) | copy-start | bytes 3076
  6.5 55.0 %copy-start.2 = (s32[1,1,256]{2,1,0:T(1,128)S(1)}, s32[1,1,256]{2,1,0:T(1,128)}, u32[]{:S(2)}) copy-start(s32[1,1,256]{2,1,0:T(1,128)} %param.13) | copy-start | bytes 3076
  6.5 50.8 %all-gather.3.cloned.1.call-start = ((), (), s32[]{:S(2)}) async-start(), calls=%async_computation.2 | async-start | bytes 2621440 | tf_op jit(solution)/shard_map/all_gather | solution.py:57
  7.3 296.4 %reduce-scatter.3.cloned.1.call-start = ((), (), s32[]{:S(2)}) async-start(), calls=%async_computation.3 | async-start | bytes 4718592 | tf_op jit(solution)/shard_map/reduce_scatter | solution.py:64
  207.1 144.6 %all-gather.5.cloned.1.call-start = ((), (), s32[]{:S(2)}) async-start(), calls=%async_computation.4 | async-start | bytes 2621440 | tf_op jit(solution)/shard_map/all_gather | solution.py:57
  305.8 292.3 %reduce-scatter.5.cloned.1.call-start = ((), (), s32[]{:S(2)}) async-start(), calls=%async_computation.5 | async-start | bytes 4718592 | tf_op jit(solution)/shard_map/reduce_scatter | solution.py:64
  495.5 104.8 %copy-start.1 = (bf16[256,256]{1,0:T(8,128)(2,1)S(1)}, bf16[256,256]{1,0:T(8,128)(2,1)}, u32[]{:S(2)}) copy-start(bf16[256,256]{1,0:T(8,128)(2,1)} %param.16) | copy-start | bytes 393220
  495.5 102.7 %copy-start.4 = (bf16[256,256]{1,0:T(8,128)(2,1)S(1)}, bf16[256,256]{1,0:T(8,128)(2,1)}, u32[]{:S(2)}) copy-start(bf16[256,256]{1,0:T(8,128)(2,1)} %param.17) | copy-start | bytes 393220
Sparse Core Ops, SparseCore 0:
  8.9 48.3 all-gather.2
  207.2 96.4 reduce-scatter.2
  306.0 45.6 all-gather.4
  501.6 96.4 reduce-scatter.4
where the time goes:
time: 608 us; the launch traced here: 607 us
  waiting for transfers between devices  280 us (46%)
  local copies, waits for them, and re-layouts  140 us (23%)
  other arithmetic  90.5 us (15%)
  matrix products  79.9 us (13%)
  between operations  16.6 us (3%)
    reduce_scatter x2, waiting for transfers between devices, propagate(): lax.psum_scatter(rounded, 'col', scatter_dimension=0, tiled=True)  193 us
    all_gather x2, waiting for transfers between devices, propagate(): lax.all_gather(inputs_now, 'row', axis=0, tiled=True)  85.8 us
    add x6, other arithmetic, group_step(): return current + placed.reshape(out_tiles, tile_size, feature_width)  66.7 us
    while x12, local copies, waits for them, and re-layouts  62.7 us
    dot_general x6, matrix products, group_step(): placed = placed + jnp.dot(selector, low, preferred_element_type=jnp.float32)  28.4 us
    dot_general x6, matrix products, group_step(): placed = jnp.dot(selector, high, preferred_element_type=jnp.float32)  26.7 us
    gather x6, local copies, waits for them, and re-layouts, group_step(): panel_tiles[source]  26.2 us
    gather x6, local copies, waits for them, and re-layouts, group_step(): values[slot_ids]  26 us
  transfers between devices with their start and end apart: 4, of which 4 were waited for; matrix products, arithmetic and copies ran while one was open for 1% of the time, Pallas kernels for 0%

commit v1 on v0

v1 whole, which is shorter than its diff:
```python
import functools

import jax
import jax.numpy as jnp
from jax import lax
from jax.experimental import pallas as pl
from jax.experimental.pallas import tpu as pltpu
from jax.sharding import PartitionSpec as P

LANES = 128
UNROLL = 8
LOADS = 4
ROWS_AT_ONCE = 256
MESH = pl.DeviceIdType.MESH


def pair_plan(row_ids, col_ids, filled, row_tiles):
    slots = row_ids.shape[0]
    pairs_total = (slots + row_tiles) // 2
    slot_ids = jnp.arange(slots, dtype=jnp.int32)
    tile_ids = jnp.arange(row_tiles, dtype=jnp.int32)
    active = slot_ids < filled
    rows = jnp.where(active, row_ids, -1)
    earlier = (rows[:, None] == rows[None, :]) & (slot_ids[None, :] < slot_ids[:, None])
    rank = jnp.sum(earlier.astype(jnp.int32), axis=1)
    hit = (rows[:, None] == tile_ids[None, :]).astype(jnp.int32)
    count = jnp.sum(hit, axis=0)
    pairs = (count + 1) // 2
    start = jnp.sum(jnp.where(tile_ids[None, :] < tile_ids[:, None], pairs[None, :], 0), axis=1)
    place = jnp.where(active, 2 * jnp.sum(hit * start[None, :], axis=1) + rank, -1)
    places = jnp.arange(2 * pairs_total, dtype=jnp.int32)
    here = (places[:, None] == place[None, :]).astype(jnp.int32)
    slot_at = slots + jnp.sum(here * (slot_ids - slots)[None, :], axis=1)
    col_at = jnp.sum(here * col_ids[None, :], axis=1)
    pair_ids = jnp.arange(pairs_total, dtype=jnp.int32)
    opens = jnp.any((pair_ids[:, None] == start[None, :]) & (count > 0)[None, :], axis=1)
    keep = jnp.where(opens, 0.0, 1.0).astype(jnp.float32)
    last = jnp.where(count > 0, start + pairs - 1, pairs_total)
    return slot_at, col_at, keep, last


def kernel(n_row, n_col, chunks, slot_at, col_at, keep, last, feat, w1, w2, vals_hbm, out, *scratch):
    phases = 2 * chunks
    panels = scratch[:phases]
    core_in = scratch[phases : 2 * phases]
    step_in = scratch[2 * phases : 3 * phases]
    vals, sums, part, agg, load_sem, g_send, g_recv, c_send, c_recv, s_send, s_recv = scratch[
        3 * phases :
    ]
    slots, tile, _ = vals_hbm.shape
    node_dev, width = feat.shape
    pairs_total = keep.shape[0]
    per_dev = node_dev // tile
    half_tiles = per_dev // 2
    n_q = n_col // 2
    steps = n_q.bit_length() - 1
    block = half_tiles * tile
    half_rows = n_q * block
    r, c = lax.axis_index("row"), lax.axis_index("col")
    b0 = lax.rem(c, 2)
    q = lax.div(c, 2)

    barrier = pltpu.get_barrier_semaphore()
    partners = []
    for bit in range(steps + 1):
        mine = lax.rem(lax.div(c, 1 << bit), 2)
        partners.append((r, c + (1 - 2 * mine) * (1 << bit)))
    for device in partners:
        pl.semaphore_signal(barrier, inc=1, device_id=device, device_id_type=MESH)

    @pl.when(r > 0)
    def _():
        pl.semaphore_signal(barrier, inc=1, device_id=(r - 1, c), device_id_type=MESH)

    @pl.when(r < n_row - 1)
    def _():
        pl.semaphore_signal(barrier, inc=1, device_id=(r + 1, c), device_id_type=MESH)

    share = slots // LOADS
    loads = [
        pltpu.make_async_copy(
            vals_hbm.at[pl.ds(i * share, share)], vals.at[pl.ds(i * share, share)], load_sem.at[i]
        )
        for i in range(LOADS)
    ]
    for load in loads:
        load.start()

    def own(phase, offset, rows):
        return panels[phase].at[pl.ds(r * per_dev + offset, rows)]

    def project(chunk):
        def body(i, carry):
            at = pl.multiple_of(i * ROWS_AT_ONCE, ROWS_AT_ONCE)
            product = jnp.dot(
                feat[pl.ds(at, ROWS_AT_ONCE), :],
                w1[:, chunk * LANES : (chunk + 1) * LANES],
                preferred_element_type=jnp.float32,
            )
            tiles = ROWS_AT_ONCE // tile
            own(chunk, i * tiles, tiles)[...] = product.astype(jnp.bfloat16).reshape(
                tiles, tile, LANES
            )
            return carry

        lax.fori_loop(0, node_dev // ROWS_AT_ONCE, body, 0)

    project(0)
    neighbours = (r > 0).astype(jnp.int32) + (r < n_row - 1).astype(jnp.int32)
    pl.semaphore_wait(barrier, len(partners) + neighbours)

    def hop_copy(phase, way, hop, node, device):
        view = panels[phase].at[pl.ds(node * per_dev, per_dev)]
        return pltpu.make_async_remote_copy(
            src_ref=view,
            dst_ref=view,
            send_sem=g_send.at[phase, way, hop - 1],
            recv_sem=g_recv.at[phase, way, hop - 1],
            device_id=(device, c),
            device_id_type=MESH,
        )

    def sends(phase, hop):
        yield (r < n_row - 1) & (r >= hop - 1), lambda: hop_copy(phase, 0, hop, r - hop + 1, r + 1)
        yield (r > 0) & (r + hop <= n_row), lambda: hop_copy(phase, 1, hop, r + hop - 1, r - 1)

    def hop_start(phase, hop):
        for cond, make in sends(phase, hop):

            @pl.when(cond)
            def _(make=make):
                make().start()

    def hop_wait(phase, hop):
        @pl.when(r >= hop)
        def _():
            hop_copy(phase, 0, hop, r - hop, r).wait_recv()

        @pl.when(r + hop < n_row)
        def _():
            hop_copy(phase, 1, hop, r + hop, r).wait_recv()

    def hop_drain(phase, hop):
        for cond, make in sends(phase, hop):

            @pl.when(cond)
            def _(make=make):
                make().wait_send()

    class Gather:
        def __init__(self, phase):
            self.phase, self.hop = phase, 0

        def advance(self):
            if self.phase >= phases or self.hop >= n_row - 1:
                return
            if self.hop > 0:
                hop_wait(self.phase, self.hop)
            self.hop += 1
            hop_start(self.phase, self.hop)

        def finish(self):
            if self.phase >= phases:
                return
            while self.hop < n_row - 1:
                self.advance()
            hop_wait(self.phase, n_row - 1)
            for hop in range(1, n_row):
                hop_drain(self.phase, hop)

    def compute(phase, low, high, total):
        panel = panels[phase]

        def one(p, acc):
            left = [vals[slot_at[2 * p + k]] for k in range(2)]
            right = [panel[col_at[2 * p + k]] for k in range(2)]
            product = jnp.dot(
                jnp.concatenate(left, axis=1),
                jnp.concatenate(right, axis=0),
                preferred_element_type=jnp.float32,
            )
            acc = acc * keep[p] + product
            sums[p] = acc.astype(jnp.bfloat16)
            return acc

        def body(i, acc):
            for u in range(UNROLL):
                acc = one(i * UNROLL + u, acc)
            return acc

        return lax.fori_loop(low // UNROLL, high // UNROLL, body, total)

    def place_rows():
        def body(i, carry):
            dest, h = lax.div(i, 2), lax.rem(i, 2)
            dq = lax.div(dest, 2)
            rev = sum(lax.rem(lax.div(dq, 1 << k), 2) * (1 << (steps - 1 - k)) for k in range(steps))
            at = rev * (1 - h) + dq * h
            base = ((lax.rem(dest, 2) * 2 + h) * n_q + at) * half_tiles
            for t in range(half_tiles):
                row_tile = dest * per_dev + h * half_tiles + t
                part[pl.ds(pl.multiple_of((base + t) * tile, tile), tile), :] = sums[last[row_tile]]
            return carry

        lax.fori_loop(0, 2 * n_col, body, 0)

    def add_in(at, source, source_at, rows):
        piece = min(rows, ROWS_AT_ONCE)

        def body(i, carry):
            here = pl.ds(pl.multiple_of(at + i * piece, tile), piece)
            there = pl.ds(pl.multiple_of(source_at + i * piece, tile), piece)
            added = part[here, :].astype(jnp.float32) + source[there, :].astype(jnp.float32)
            part[here, :] = added.astype(jnp.bfloat16)
            return carry

        lax.fori_loop(0, rows // piece, body, 0)

    def remote(src, dst, send_sem, recv_sem, device):
        return pltpu.make_async_remote_copy(
            src_ref=src,
            dst_ref=dst,
            send_sem=send_sem,
            recv_sem=recv_sem,
            device_id=device,
            device_id_type=MESH,
        )

    def rows_at(ref, at, rows):
        return ref.at[pl.ds(pl.multiple_of(at, tile), rows)]

    def reduce(phase, gather):
        first = [
            remote(
                rows_at(part, ((1 - b0) * 2 + h) * half_rows, half_rows),
                core_in[phase].at[pl.ds(h * half_rows, half_rows)],
                c_send.at[phase, h],
                c_recv.at[phase, h],
                partners[0],
            )
            for h in range(2)
        ]
        started = list(first)
        for copy in first:
            copy.start()
        gather.advance()
        base = [(b0 * 2 + h) * half_rows for h in range(2)]
        size = half_rows
        arrived = [(first[h], core_in[phase], h * half_rows) for h in range(2)]
        for step in range(steps):
            following = []
            for h in range(2):
                copy, source, source_at = arrived[h]
                copy.wait_recv()
                add_in(base[h], source, source_at, size)
                bit = step if h == 0 else steps - 1 - step
                mine = lax.rem(lax.div(q, 1 << bit), 2)
                landing = (h * (n_q - 1) + n_q - (n_q >> step)) * block
                copy = remote(
                    rows_at(part, base[h] + (1 - mine) * (size // 2), size // 2),
                    step_in[phase].at[pl.ds(landing, size // 2)],
                    s_send.at[phase, h, step],
                    s_recv.at[phase, h, step],
                    partners[1 + bit],
                )
                copy.start()
                started.append(copy)
                base[h] = base[h] + mine * (size // 2)
                following.append((copy, step_in[phase], landing))
            size //= 2
            arrived = following
            gather.advance()
        for h in range(2):
            copy, source, source_at = arrived[h]
            copy.wait_recv()
            here = pl.ds(pl.multiple_of(base[h], tile), block)
            added = part[here, :].astype(jnp.float32) + source[
                pl.ds(source_at, block), :
            ].astype(jnp.float32)
            if phase < chunks:
                hidden = jnp.maximum(added, 0.0).astype(jnp.bfloat16)
                own(phase + chunks, h * half_tiles, half_tiles)[...] = hidden.reshape(
                    half_tiles, tile, LANES
                )
            else:
                agg[phase - chunks, pl.ds(h * block, block), :] = added.astype(jnp.bfloat16)
        for copy in started:
            copy.wait_send()

    vals[slots] = jnp.zeros((tile, tile), vals.dtype)
    sums[pairs_total] = jnp.zeros((tile, LANES), sums.dtype)
    gather = Gather(0)
    gather.advance()
    for chunk in range(1, chunks):
        project(chunk)
    for load in loads:
        load.wait()
    gather.finish()
    for phase in range(phases):
        gather = Gather(phase + 1)
        gather.advance()
        total = jnp.zeros((tile, LANES), jnp.float32)
        compute(phase, 0, pairs_total, total)
        place_rows()
        reduce(phase, gather)
        gather.finish()

    def finish(i, carry):
        here = pl.ds(pl.multiple_of(i * ROWS_AT_ONCE, ROWS_AT_ONCE), ROWS_AT_ONCE)
        whole = jnp.concatenate([agg[chunk, here, :] for chunk in range(chunks)], axis=1)
        product = jnp.dot(whole, w2[...], preferred_element_type=jnp.float32)
        out[here, :] = jnp.maximum(product, 0.0).astype(out.dtype)
        return carry

    lax.fori_loop(0, node_dev // ROWS_AT_ONCE, finish, 0)


def shards(n_row, n_col, features, tile_values, tile_rows, tile_cols, tile_count, w_first, w_second):
    slots, tile = tile_values.shape[2], tile_values.shape[-1]
    node_dev, width = features.shape
    row_tiles = node_dev * n_col // tile
    chunks = width // LANES
    phases = 2 * chunks
    pairs_total = (slots + row_tiles) // 2
    n_q = n_col // 2
    steps = n_q.bit_length() - 1
    plan = pair_plan(tile_rows[0, 0], tile_cols[0, 0], tile_count[0, 0], row_tiles)
    half = node_dev // 2
    vmem = pl.BlockSpec(memory_space=pltpu.VMEM)
    smem = pl.BlockSpec(memory_space=pltpu.SMEM)
    bf16 = jnp.bfloat16
    dma = pltpu.SemaphoreType.DMA
    return pl.pallas_call(
        functools.partial(kernel, n_row, n_col, chunks),
        name="gcn",
        out_shape=jax.ShapeDtypeStruct((node_dev, width), bf16),
        in_specs=[smem] * 4 + [vmem] * 3 + [pl.BlockSpec(memory_space=pltpu.HBM)],
        out_specs=vmem,
        scratch_shapes=[pltpu.VMEM((n_row * node_dev // tile, tile, LANES), bf16)] * phases
        + [pltpu.VMEM((2 * n_q * half, LANES), bf16)] * phases
        + [pltpu.VMEM((2 * (n_q - 1) * half, LANES), bf16)] * phases
        + [
            pltpu.VMEM((slots + 1, tile, tile), bf16),
            pltpu.VMEM((pairs_total + 1, tile, LANES), bf16),
            pltpu.VMEM((n_col * node_dev, LANES), bf16),
            pltpu.VMEM((chunks, node_dev, LANES), bf16),
            dma((LOADS,)),
            dma((phases, 2, n_row - 1)),
            dma((phases, 2, n_row - 1)),
            dma((phases, 2)),
            dma((phases, 2)),
            dma((phases, 2, steps)),
            dma((phases, 2, steps)),
        ],
        compiler_params=pltpu.CompilerParams(
            collective_id=0, has_side_effects=True, vmem_limit_bytes=63 * 1024 * 1024
        ),
    )(*plan, features, w_first, w_second, tile_values[0, 0])


def solution(mesh):
    return jax.shard_map(
        functools.partial(shards, mesh.shape["row"], mesh.shape["col"]),
        mesh=mesh,
        in_specs=(
            P(("row", "col"), None),
            P("row", "col", None, None, None),
            P("row", "col", None),
            P("row", "col", None),
            P("row", "col"),
            P(),
            P(),
        ),
        out_specs=P(("row", "col"), None),
        check_vma=False,
    )
```

time: 608 us -> 118 us (0.19)
  waiting for transfers between devices: 280 us -> 0 us
  local copies, waits for them, and re-layouts: 140 us -> 1.87 us
  Pallas kernels: 0 us -> 111 us
  other arithmetic: 90.5 us -> 4.5 us
  matrix products: 79.9 us -> 0 us
  between operations: 16.6 us -> 0.68 us
    reduce_scatter x2 -> x0, waiting for transfers between devices: 193 us -> none  [propagate(): lax.psum_scatter(rounded, 'col', scatter_dimension=0, tiled=True)]
    pallas_call x0 -> x1, Pallas kernels: none -> 111 us  [shards(): pl.pallas_call(functools.partial(kernel, n_row, n_col, chunks), name='gcn...]
    all_gather x2 -> x0, waiting for transfers between devices: 85.8 us -> none  [propagate(): lax.all_gather(inputs_now, 'row', axis=0, tiled=True)]
    dot_general x20 -> x0, matrix products: 79.9 us -> none  [the longest x6 28.4 us: group_step(): placed = placed + jnp.dot(selector, low, preferred_element_type=jnp.float32)]
    gather x31 -> x0, local copies, waits for them, and re-layouts: 68.4 us -> none  [the longest x6 26.2 us: group_step(): panel_tiles[source]]
    add x6 -> x1, other arithmetic: 66.7 us -> 0.59 us  [pair_plan(): slot_at = slots + jnp.sum(here * (slot_ids - slots)[None, :], axis=1)]
    while x12 -> x0, local copies, waits for them, and re-layouts: 62.7 us -> none
    convert_element_type x2 -> x0, other arithmetic: 12 us -> none  [propagate(): rounded = partial_value.reshape(-1, feature_width).astype(jnp.bfloat16)]
  transfers between devices with their start and end apart: 4 -> 0, of which waited for: 4 -> 0; matrix products, arithmetic and copies ran while one was open for 1% -> 0% of each run, Pallas kernels for 0% -> 0%
where the time goes in v1:
time: 118 us
  Pallas kernels  111 us (94%)
  other arithmetic  4.5 us (4%)
  local copies, waits for them, and re-layouts  1.87 us (2%)
    pallas_call x1, Pallas kernels, shards(): pl.pallas_call(functools.partial(kernel, n_row, n_col, chunks), name='gcn...  111 us

profile of v1, /device:TPU:0, one launch (start us, length us, event | category | flops | bytes accessed | tf_op | source)
XLA Modules:
  0.0 118.2 jit_solution(6226988917057775962)
XLA Ops:
  0.7 0.7 fusion.3
  1.3 0.1 convert_reduce_fusion.1
  1.5 0.1 select_reduce_fusion.3
  1.6 0.6 add_select_fusion.1.last
  2.2 0.1 fusion.2
  2.3 0.1 select_reduce_fusion.2
  2.4 0.2 convert_reduce_fusion
  2.6 0.6 broadcast_select_fusion.keep
  3.1 1.5 %select_reduce_fusion = (s32[320]{0:T(512)}, s32[320]{0:T(512)S(1)}) fusion(s32[256]{0:T(256)} %bitcast.7, s32[256]{0:T(256)S(1)} %get-tuple-element.8, s32[256]{0:T(256)S(1)} %get-tuple-element.7), kind=kLoop, calls=%fused_computation | loop fusion | flops 408960 | bytes 5632 | tf_op jit(solution)/shard_map/reduce_sum | solution.py:34
  4.6 0.6 broadcast_add_fusion.slot_at
  5.2 111.1 %gcn.1 = bf16[1024,256]{1,0:T(8,128)(2,1)} custom-call(s32[320]{0:T(512)} %broadcast_add_fusion.slot_at, s32[320]{0:T(512)} %get-tuple-element.5.col_at, f32[160]{0:T(256)} %broadcast_select_fusion.keep, s32[64]{0:T(128)} %add_select_fusion.1.last, bf16[1024,256]{1,0:T(8,128)(2,1)} %feat.1, bf16[256,256]{1,0:T(8,128)(2,1)} %w1.1, bf16[256,256]{1,0:T(8,128)(2,1)} %w2.1, ...), custom_call_target="tpu_custom_call" | custom-call | tf_op jit(solution)/shard_map/gcn/pallas_call | solution.py:333
  116.3 1.9 %copy.10 = bf16[1024,256]{1,0:T(8,128)(2,1)} copy(bf16[1024,256]{1,0:T(8,128)(2,1)} %gcn.1) | data formatting | bytes 1048576
  (3 shorter events, 0.0 us)

commit v2 on v1

--- a/solution.py
+++ b/solution.py
@@ -14,42 +14,53 @@
 MESH = pl.DeviceIdType.MESH
 
 
-def pair_plan(row_ids, col_ids, filled, row_tiles):
-    slots = row_ids.shape[0]
-    pairs_total = (slots + row_tiles) // 2
-    slot_ids = jnp.arange(slots, dtype=jnp.int32)
-    tile_ids = jnp.arange(row_tiles, dtype=jnp.int32)
-    active = slot_ids < filled
-    rows = jnp.where(active, row_ids, -1)
-    earlier = (rows[:, None] == rows[None, :]) & (slot_ids[None, :] < slot_ids[:, None])
-    rank = jnp.sum(earlier.astype(jnp.int32), axis=1)
-    hit = (rows[:, None] == tile_ids[None, :]).astype(jnp.int32)
-    count = jnp.sum(hit, axis=0)
-    pairs = (count + 1) // 2
-    start = jnp.sum(jnp.where(tile_ids[None, :] < tile_ids[:, None], pairs[None, :], 0), axis=1)
-    place = jnp.where(active, 2 * jnp.sum(hit * start[None, :], axis=1) + rank, -1)
-    places = jnp.arange(2 * pairs_total, dtype=jnp.int32)
-    here = (places[:, None] == place[None, :]).astype(jnp.int32)
-    slot_at = slots + jnp.sum(here * (slot_ids - slots)[None, :], axis=1)
-    col_at = jnp.sum(here * col_ids[None, :], axis=1)
-    pair_ids = jnp.arange(pairs_total, dtype=jnp.int32)
-    opens = jnp.any((pair_ids[:, None] == start[None, :]) & (count > 0)[None, :], axis=1)
-    keep = jnp.where(opens, 0.0, 1.0).astype(jnp.float32)
-    last = jnp.where(count > 0, start + pairs - 1, pairs_total)
-    return slot_at, col_at, keep, last
-
-
-def kernel(n_row, n_col, chunks, slot_at, col_at, keep, last, feat, w1, w2, vals_hbm, out, *scratch):
+def iota(shape, axis):
+    return lax.broadcasted_iota(jnp.int32, shape, axis)
+
+
+def pair_plan(row_ids, col_ids, filled, row_tiles, pairs_total, width):
+    slots = row_ids.shape[1]
+    one, zero = jnp.int32(1), jnp.int32(0)
+
+    def down(mask):
+        return jnp.sum(mask, axis=0, keepdims=True)
+
+    def across(mask):
+        return jnp.sum(mask, axis=1, keepdims=True)
+
+    square = (slots, slots)
+    lane, sub = iota(square, 1), iota(square, 0)
+    rows_l = jnp.where(iota((1, slots), 1) < filled, row_ids, -1)
+    rows_s = across(jnp.where(lane == sub, rows_l, zero))
+    cols_s = across(jnp.where(lane == sub, col_ids, zero))
+    rank_s = across(jnp.where((rows_s == rows_l) & (lane < sub), one, zero))
+    hit = jnp.where(rows_s == iota((slots, row_tiles), 1), one, zero)
+    hit_t = jnp.where(rows_l == iota((row_tiles, slots), 0), one, zero)
+    count_l, count_s = down(hit), across(hit_t)
+    pairs_l, pairs_s = (count_l + 1) >> 1, (count_s + 1) >> 1
+    box = (row_tiles, row_tiles)
+    start_l = down(jnp.where(iota(box, 0) < iota(box, 1), pairs_s, zero))
+    start_s = across(jnp.where(iota(box, 1) < iota(box, 0), pairs_l, zero))
+    place_s = jnp.where(rows_s >= 0, 2 * across(hit * start_l) + rank_s, -one)
+    here = place_s == iota((slots, width), 1)
+    slot_ids = iota((slots, width), 0)
+    slot_at = slots + down(jnp.where(here, slot_ids - slots, zero))
+    col_at = down(jnp.where(here, cols_s, zero))
+    opens = (start_s == iota((row_tiles, width), 1)) & (count_s > 0)
+    keep = one - down(jnp.where(opens, one, zero))
+    last = jnp.where(count_l > 0, start_l + pairs_l - 1, jnp.int32(pairs_total))
+    return slot_at, col_at, keep.astype(jnp.float32), last
+
+
+def kernel(n_row, n_col, chunks, pairs_total, filled, row_ids, col_ids, feat, w1, vals_hbm, out, *scratch):
     phases = 2 * chunks
     panels = scratch[:phases]
     core_in = scratch[phases : 2 * phases]
     step_in = scratch[2 * phases : 3 * phases]
-    vals, sums, part, agg, load_sem, g_send, g_recv, c_send, c_recv, s_send, s_recv = scratch[
-        3 * phases :
-    ]
+    vals, sums, part, plan_v, keep_v, plan, keep, plan_sem = scratch[3 * phases : 3 * phases + 8]
+    load_sem, g_send, g_recv, c_send, c_recv, s_send, s_recv = scratch[3 * phases + 8 :]
     slots, tile, _ = vals_hbm.shape
     node_dev, width = feat.shape
-    pairs_total = keep.shape[0]
     per_dev = node_dev // tile
     half_tiles = per_dev // 2
     n_q = n_col // 2
@@ -172,14 +183,14 @@
         panel = panels[phase]
 
         def one(p, acc):
-            left = [vals[slot_at[2 * p + k]] for k in range(2)]
-            right = [panel[col_at[2 * p + k]] for k in range(2)]
+            left = [vals[plan[0, 2 * p + k]] for k in range(2)]
+            right = [panel[plan[1, 2 * p + k]] for k in range(2)]
             product = jnp.dot(
                 jnp.concatenate(left, axis=1),
                 jnp.concatenate(right, axis=0),
                 preferred_element_type=jnp.float32,
             )
-            acc = acc * keep[p] + product
+            acc = acc * keep[0, p] + product
             sums[p] = acc.astype(jnp.bfloat16)
             return acc
 
@@ -190,19 +201,21 @@
 
         return lax.fori_loop(low // UNROLL, high // UNROLL, body, total)
 
-    def place_rows():
+    def place_rows(parity):
         def body(i, carry):
-            dest, h = lax.div(i, 2), lax.rem(i, 2)
-            dq = lax.div(dest, 2)
+            dq, h = lax.div(i, 2), lax.rem(i, 2)
+            dest = 2 * dq + parity
             rev = sum(lax.rem(lax.div(dq, 1 << k), 2) * (1 << (steps - 1 - k)) for k in range(steps))
             at = rev * (1 - h) + dq * h
-            base = ((lax.rem(dest, 2) * 2 + h) * n_q + at) * half_tiles
+            base = ((parity * 2 + h) * n_q + at) * half_tiles
             for t in range(half_tiles):
                 row_tile = dest * per_dev + h * half_tiles + t
-                part[pl.ds(pl.multiple_of((base + t) * tile, tile), tile), :] = sums[last[row_tile]]
+                part[pl.ds(pl.multiple_of((base + t) * tile, tile), tile), :] = sums[
+                    plan[2, row_tile]
+                ]
             return carry
 
-        lax.fori_loop(0, 2 * n_col, body, 0)
+        lax.fori_loop(0, 2 * n_q, body, 0)
 
     def add_in(at, source, source_at, rows):
         piece = min(rows, ROWS_AT_ONCE)
@@ -229,63 +242,82 @@
     def rows_at(ref, at, rows):
         return ref.at[pl.ds(pl.multiple_of(at, tile), rows)]
 
+    def mine_at(h, step):
+        return lax.rem(lax.div(q, 1 << (step if h == 0 else steps - 1 - step)), 2)
+
+    def pieces(h, step, size):
+        if step >= steps:
+            return [(0, size)]
+        mine = mine_at(h, step)
+        return [((1 - mine) * (size // 2), size // 2), (mine * (size // 2), size // 2)]
+
     def reduce(phase, gather):
-        first = [
-            remote(
-                rows_at(part, ((1 - b0) * 2 + h) * half_rows, half_rows),
-                core_in[phase].at[pl.ds(h * half_rows, half_rows)],
-                c_send.at[phase, h],
-                c_recv.at[phase, h],
-                partners[0],
-            )
-            for h in range(2)
-        ]
-        started = list(first)
-        for copy in first:
-            copy.start()
-        gather.advance()
-        base = [(b0 * 2 + h) * half_rows for h in range(2)]
-        size = half_rows
-        arrived = [(first[h], core_in[phase], h * half_rows) for h in range(2)]
-        for step in range(steps):
-            following = []
+        place_rows(1 - b0)
+        started = []
+        cuts = [pieces(h, 0, half_rows) for h in range(2)]
+        arrived = [[], []]
+        for k in range(len(cuts[0])):
             for h in range(2):
-                copy, source, source_at = arrived[h]
-                copy.wait_recv()
-                add_in(base[h], source, source_at, size)
-                bit = step if h == 0 else steps - 1 - step
-                mine = lax.rem(lax.div(q, 1 << bit), 2)
-                landing = (h * (n_q - 1) + n_q - (n_q >> step)) * block
+                off, rows = cuts[h][k]
                 copy = remote(
-                    rows_at(part, base[h] + (1 - mine) * (size // 2), size // 2),
-                    step_in[phase].at[pl.ds(landing, size // 2)],
-                    s_send.at[phase, h, step],
-                    s_recv.at[phase, h, step],
-                    partners[1 + bit],
+                    rows_at(part, ((1 - b0) * 2 + h) * half_rows + off, rows),
+                    rows_at(core_in[phase], h * half_rows + off, rows),
+                    c_send.at[phase, h, k],
+                    c_recv.at[phase, h, k],
+                    partners[0],
                 )
                 copy.start()
                 started.append(copy)
-                base[h] = base[h] + mine * (size // 2)
-                following.append((copy, step_in[phase], landing))
+                arrived[h].append((copy, core_in[phase], h * half_rows + off, off, rows))
+        place_rows(b0)
+        gather.advance()
+        base = [(b0 * 2 + h) * half_rows for h in range(2)]
+
+        def take(h, k):
+            copy, source, source_at, off, rows = arrived[h][k]
+            copy.wait_recv()
+            add_in(base[h] + off, source, source_at, rows)
+
+        size = half_rows
+        for step in range(steps):
+            following = [[], []]
+            for h in range(2):
+                take(h, 0)
+                bit = step if h == 0 else steps - 1 - step
+                away = base[h] + (1 - mine_at(h, step)) * (size // 2)
+                landing = (h * (n_q - 1) + n_q - (n_q >> step)) * block
+                for k, (off, rows) in enumerate(pieces(h, step + 1, size // 2)):
+                    copy = remote(
+                        rows_at(part, away + off, rows),
+                        rows_at(step_in[phase], landing + off, rows),
+                        s_send.at[phase, h, step, k],
+                        s_recv.at[phase, h, step, k],
+                        partners[1 + bit],
+                    )
+                    copy.start()
+                    started.append(copy)
+                    following[h].append((copy, step_in[phase], landing + off, off, rows))
+            for h in range(2):
+                take(h, 1)
+                base[h] = base[h] + mine_at(h, step) * (size // 2)
             size //= 2
             arrived = following
             gather.advance()
         for h in range(2):
-            copy, source, source_at = arrived[h]
+            copy, source, source_at, off, rows = arrived[h][0]
             copy.wait_recv()
             here = pl.ds(pl.multiple_of(base[h], tile), block)
-            added = part[here, :].astype(jnp.float32) + source[
-                pl.ds(source_at, block), :
-            ].astype(jnp.float32)
+            there = pl.ds(pl.multiple_of(source_at, tile), block)
+            added = part[here, :].astype(jnp.float32) + source[there, :].astype(jnp.float32)
             if phase < chunks:
                 hidden = jnp.maximum(added, 0.0).astype(jnp.bfloat16)
                 own(phase + chunks, h * half_tiles, half_tiles)[...] = hidden.reshape(
                     half_tiles, tile, LANES
                 )
             else:
-                agg[phase - chunks, pl.ds(h * block, block), :] = added.astype(jnp.bfloat16)
-        for copy in started:
-            copy.wait_send()
+                at = (phase - chunks) * LANES
+                out[h * block : (h + 1) * block, at : at + LANES] = added.astype(jnp.bfloat16)
+        return started
 
     vals[slots] = jnp.zeros((tile, tile), vals.dtype)
     sums[pairs_total] = jnp.zeros((tile, LANES), sums.dtype)
@@ -293,26 +325,39 @@
     gather.advance()
     for chunk in range(1, chunks):
         project(chunk)
+    slot_at, col_at, keep_at, last = pair_plan(
+        row_ids[...], col_ids[...], filled[0, 0], n_col * per_dev, pairs_total, plan.shape[1]
+    )
+    plan_v[0:1, :] = slot_at
+    plan_v[1:2, :] = col_at
+    plan_v[2:3, : last.shape[1]] = last
+    keep_v[0:1, :] = keep_at
+    moves = [
+        pltpu.make_async_copy(plan_v, plan, plan_sem.at[0]),
+        pltpu.make_async_copy(keep_v, keep, plan_sem.at[1]),
+    ]
+    gather.advance()
+    for move in moves:
+        move.start()
+    for move in moves:
+        move.wait()
     for load in loads:
         load.wait()
+    following = Gather(1)
+    while gather.hop < n_row - 1:
+        gather.advance()
+    following.advance()
     gather.finish()
     for phase in range(phases):
-        gather = Gather(phase + 1)
-        gather.advance()
-        total = jnp.zeros((tile, LANES), jnp.float32)
-        compute(phase, 0, pairs_total, total)
-        place_rows()
-        reduce(phase, gather)
+        gather, following = following, Gather(phase + 2)
+        compute(phase, 0, pairs_total, jnp.zeros((tile, LANES), jnp.float32))
+        started = reduce(phase, gather)
+        while gather.phase < phases and gather.hop < n_row - 1:
+            gather.advance()
+        following.advance()
+        for copy in started:
+            copy.wait_send()
         gather.finish()
-
-    def finish(i, carry):
-        here = pl.ds(pl.multiple_of(i * ROWS_AT_ONCE, ROWS_AT_ONCE), ROWS_AT_ONCE)
-        whole = jnp.concatenate([agg[chunk, here, :] for chunk in range(chunks)], axis=1)
-        product = jnp.dot(whole, w2[...], preferred_element_type=jnp.float32)
-        out[here, :] = jnp.maximum(product, 0.0).astype(out.dtype)
-        return carry
-
-    lax.fori_loop(0, node_dev // ROWS_AT_ONCE, finish, 0)
 
 
 def shards(n_row, n_col, features, tile_values, tile_rows, tile_cols, tile_count, w_first, w_second):
@@ -324,17 +369,17 @@
     pairs_total = (slots + row_tiles) // 2
     n_q = n_col // 2
     steps = n_q.bit_length() - 1
-    plan = pair_plan(tile_rows[0, 0], tile_cols[0, 0], tile_count[0, 0], row_tiles)
+    plan_width = -(-2 * pairs_total // LANES) * LANES
     half = node_dev // 2
     vmem = pl.BlockSpec(memory_space=pltpu.VMEM)
     smem = pl.BlockSpec(memory_space=pltpu.SMEM)
     bf16 = jnp.bfloat16
     dma = pltpu.SemaphoreType.DMA
-    return pl.pallas_call(
-        functools.partial(kernel, n_row, n_col, chunks),
+    aggregate = pl.pallas_call(
+        functools.partial(kernel, n_row, n_col, chunks, pairs_total),
         name="gcn",
         out_shape=jax.ShapeDtypeStruct((node_dev, width), bf16),
-        in_specs=[smem] * 4 + [vmem] * 3 + [pl.BlockSpec(memory_space=pltpu.HBM)],
+        in_specs=[smem] + [vmem] * 4 + [pl.BlockSpec(memory_space=pltpu.HBM)],
         out_specs=vmem,
         scratch_shapes=[pltpu.VMEM((n_row * node_dev // tile, tile, LANES), bf16)] * phases
         + [pltpu.VMEM((2 * n_q * half, LANES), bf16)] * phases
@@ -343,19 +388,25 @@
             pltpu.VMEM((slots + 1, tile, tile), bf16),
             pltpu.VMEM((pairs_total + 1, tile, LANES), bf16),
             pltpu.VMEM((n_col * node_dev, LANES), bf16),
-            pltpu.VMEM((chunks, node_dev, LANES), bf16),
+            pltpu.VMEM((8, plan_width), jnp.int32),
+            pltpu.VMEM((8, plan_width), jnp.float32),
+            pltpu.SMEM((8, plan_width), jnp.int32),
+            pltpu.SMEM((8, plan_width), jnp.float32),
+            dma((2,)),
             dma((LOADS,)),
             dma((phases, 2, n_row - 1)),
             dma((phases, 2, n_row - 1)),
-            dma((phases, 2)),
-            dma((phases, 2)),
-            dma((phases, 2, steps)),
-            dma((phases, 2, steps)),
+            dma((phases, 2, 2)),
+            dma((phases, 2, 2)),
+            dma((phases, 2, steps, 2)),
+            dma((phases, 2, steps, 2)),
         ],
         compiler_params=pltpu.CompilerParams(
             collective_id=0, has_side_effects=True, vmem_limit_bytes=63 * 1024 * 1024
         ),
-    )(*plan, features, w_first, w_second, tile_values[0, 0])
+    )(tile_count, tile_rows[0], tile_cols[0], features, w_first, tile_values[0, 0])
+    product = jnp.dot(aggregate, w_second, preferred_element_type=jnp.float32)
+    return jax.nn.relu(product).astype(bf16)
 
 
 def solution(mesh):

time: 118 us -> 108 us (0.915)
  Pallas kernels: 111 us -> 105 us
  other arithmetic: 4.5 us -> 0 us
  matrix products: 0 us -> 2.13 us
  local copies, waits for them, and re-layouts: 1.87 us -> 0.01 us
    pallas_call x1, Pallas kernels: 111 us -> 105 us  [shards(): pl.pallas_call(functools.partial(kernel, n_row, n_col, chunks, pairs_tota...]
    dot_general x0 -> x1, matrix products: none -> 2.13 us  [shards(): product = jnp.dot(aggregate, w_second, preferred_element_type=jnp.float32)]
    reduce_sum x5 -> x0, other arithmetic: 1.94 us -> none  [the longest x1 1.45 us: pair_plan(): col_at = jnp.sum(here * col_ids[None, :], axis=1)]
    unnamed x1 -> x2, local copies, waits for them, and re-layouts: 1.87 us -> 0.01 us
    select_n x4 -> x0, other arithmetic: 1.85 us -> none  [the longest x1 0.68 us: pair_plan(): rows = jnp.where(active, row_ids, -1)]
where the time goes in v2:
time: 108 us
  Pallas kernels  105 us (97%)
  matrix products  2.13 us (2%)
    pallas_call x1, Pallas kernels, shards(): pl.pallas_call(functools.partial(kernel, n_row, n_col, chunks, pairs_tota...  105 us

profile of v2, /device:TPU:0, one launch (start us, length us, event | category | flops | bytes accessed | tf_op | source)
XLA Modules:
  0.0 108.1 jit_solution(9134966211925095724)
XLA Ops:
  0.0 0.0 copy-start
  0.7 105.3 %gcn.1 = bf16[1024,256]{1,0:T(8,128)(2,1)} custom-call(s32[1,1]{1,0:T(1,128)S(6)} %copy.8.filled, s32[1,256]{1,0:T(1,128)} %bitcast.6, s32[1,256]{1,0:T(1,128)} %bitcast.7, bf16[1024,256]{1,0:T(8,128)(2,1)} %feat.1, bf16[256,256]{1,0:T(8,128)(2,1)} %w1.1, bf16[256,128,128]{2,1,0:T(8,128)(2,1)} %bitcast.5), custom_call_target="tpu_custom_call" | custom-call | tf_op jit(solution)/shard_map/gcn/pallas_call | solution.py:378
  106.0 0.0 copy-done
  106.0 2.1 %fusion = bf16[1024,256]{1,0:T(8,128)(2,1)} fusion(bf16[1024,256]{1,0:T(8,128)(2,1)} %gcn.1, bf16[256,256]{1,0:T(8,128)(2,1)S(1)} %copy-done), kind=kOutput, calls=%fused_computation.1 | convolution fusion | flops 134742016 | bytes 1179648 | tf_op jit(solution)/shard_map/dot_general | solution.py:408
Async XLA Ops:
  0.0 106.0 %copy-start = (bf16[256,256]{1,0:T(8,128)(2,1)S(1)}, bf16[256,256]{1,0:T(8,128)(2,1)}, u32[]{:S(2)}) copy-start(bf16[256,256]{1,0:T(8,128)(2,1)} %param.13) | copy-start | bytes 393220

commit v3 on v2

--- a/solution.py
+++ b/solution.py
@@ -10,6 +10,7 @@
 LANES = 128
 UNROLL = 8
 LOADS = 4
+PARTS = 2
 ROWS_AT_ONCE = 256
 MESH = pl.DeviceIdType.MESH
 
@@ -120,39 +121,43 @@
     neighbours = (r > 0).astype(jnp.int32) + (r < n_row - 1).astype(jnp.int32)
     pl.semaphore_wait(barrier, len(partners) + neighbours)
 
-    def hop_copy(phase, way, hop, node, device):
-        view = panels[phase].at[pl.ds(node * per_dev, per_dev)]
+    cut = per_dev // PARTS
+
+    def hop_copy(phase, way, hop, part_id, node, device):
+        view = panels[phase].at[pl.ds(node * per_dev + part_id * cut, cut)]
         return pltpu.make_async_remote_copy(
             src_ref=view,
             dst_ref=view,
-            send_sem=g_send.at[phase, way, hop - 1],
-            recv_sem=g_recv.at[phase, way, hop - 1],
+            send_sem=g_send.at[phase, way, hop - 1, part_id],
+            recv_sem=g_recv.at[phase, way, hop - 1, part_id],
             device_id=(device, c),
             device_id_type=MESH,
         )
 
-    def sends(phase, hop):
-        yield (r < n_row - 1) & (r >= hop - 1), lambda: hop_copy(phase, 0, hop, r - hop + 1, r + 1)
-        yield (r > 0) & (r + hop <= n_row), lambda: hop_copy(phase, 1, hop, r + hop - 1, r - 1)
-
-    def hop_start(phase, hop):
-        for cond, make in sends(phase, hop):
+    def sends(phase, hop, k):
+        yield (r < n_row - 1) & (r >= hop - 1), lambda: hop_copy(
+            phase, 0, hop, k, r - hop + 1, r + 1
+        )
+        yield (r > 0) & (r + hop <= n_row), lambda: hop_copy(phase, 1, hop, k, r + hop - 1, r - 1)
+
+    def hop_start(phase, hop, k):
+        for cond, make in sends(phase, hop, k):
 
             @pl.when(cond)
             def _(make=make):
                 make().start()
 
-    def hop_wait(phase, hop):
+    def hop_wait(phase, hop, k):
         @pl.when(r >= hop)
         def _():
-            hop_copy(phase, 0, hop, r - hop, r).wait_recv()
+            hop_copy(phase, 0, hop, k, r - hop, r).wait_recv()
 
         @pl.when(r + hop < n_row)
         def _():
-            hop_copy(phase, 1, hop, r + hop, r).wait_recv()
-
-    def hop_drain(phase, hop):
-        for cond, make in sends(phase, hop):
+            hop_copy(phase, 1, hop, k, r + hop, r).wait_recv()
+
+    def hop_drain(phase, hop, k):
+        for cond, make in sends(phase, hop, k):
 
             @pl.when(cond)
             def _(make=make):
@@ -160,24 +165,28 @@
 
     class Gather:
         def __init__(self, phase):
-            self.phase, self.hop = phase, 0
-
-        def advance(self):
-            if self.phase >= phases or self.hop >= n_row - 1:
-                return
-            if self.hop > 0:
-                hop_wait(self.phase, self.hop)
-            self.hop += 1
-            hop_start(self.phase, self.hop)
+            self.phase, self.unit = phase, 0
+            self.units = (n_row - 1) * PARTS if phase < phases else 0
+
+        def advance(self, count=1):
+            for _ in range(min(count, self.units - self.unit)):
+                hop, k = self.unit // PARTS + 1, self.unit % PARTS
+                if hop > 1:
+                    hop_wait(self.phase, hop - 1, k)
+                hop_start(self.phase, hop, k)
+                self.unit += 1
+
+        def send_all(self):
+            self.advance(self.units)
 
         def finish(self):
-            if self.phase >= phases:
-                return
-            while self.hop < n_row - 1:
-                self.advance()
-            hop_wait(self.phase, n_row - 1)
-            for hop in range(1, n_row):
-                hop_drain(self.phase, hop)
+            self.send_all()
+            if self.units:
+                for k in range(PARTS):
+                    hop_wait(self.phase, n_row - 1, k)
+                for hop in range(1, n_row):
+                    for k in range(PARTS):
+                        hop_drain(self.phase, hop, k)
 
     def compute(phase, low, high, total):
         panel = panels[phase]
@@ -269,6 +278,7 @@
                 copy.start()
                 started.append(copy)
                 arrived[h].append((copy, core_in[phase], h * half_rows + off, off, rows))
+        gather.advance()
         place_rows(b0)
         gather.advance()
         base = [(b0 * 2 + h) * half_rows for h in range(2)]
@@ -322,7 +332,7 @@
     vals[slots] = jnp.zeros((tile, tile), vals.dtype)
     sums[pairs_total] = jnp.zeros((tile, LANES), sums.dtype)
     gather = Gather(0)
-    gather.advance()
+    gather.advance(PARTS)
     for chunk in range(1, chunks):
         project(chunk)
     slot_at, col_at, keep_at, last = pair_plan(
@@ -336,7 +346,7 @@
         pltpu.make_async_copy(plan_v, plan, plan_sem.at[0]),
         pltpu.make_async_copy(keep_v, keep, plan_sem.at[1]),
     ]
-    gather.advance()
+    gather.advance(PARTS)
     for move in moves:
         move.start()
     for move in moves:
@@ -344,17 +354,18 @@
     for load in loads:
         load.wait()
     following = Gather(1)
-    while gather.hop < n_row - 1:
-        gather.advance()
-    following.advance()
+    gather.send_all()
+    following.advance(PARTS)
     gather.finish()
     for phase in range(phases):
         gather, following = following, Gather(phase + 2)
-        compute(phase, 0, pairs_total, jnp.zeros((tile, LANES), jnp.float32))
+        middle = pairs_total // 2 // UNROLL * UNROLL
+        total = compute(phase, 0, middle, jnp.zeros((tile, LANES), jnp.float32))
+        gather.advance()
+        compute(phase, middle, pairs_total, total)
         started = reduce(phase, gather)
-        while gather.phase < phases and gather.hop < n_row - 1:
-            gather.advance()
-        following.advance()
+        gather.send_all()
+        following.advance(PARTS)
         for copy in started:
             copy.wait_send()
         gather.finish()
@@ -394,8 +405,8 @@
             pltpu.SMEM((8, plan_width), jnp.float32),
             dma((2,)),
             dma((LOADS,)),
-            dma((phases, 2, n_row - 1)),
-            dma((phases, 2, n_row - 1)),
+            dma((phases, 2, n_row - 1, PARTS)),
+            dma((phases, 2, n_row - 1, PARTS)),
             dma((phases, 2, 2)),
             dma((phases, 2, 2)),
             dma((phases, 2, steps, 2)),

time: 108 us -> 108 us (level)
  no operation moved by 1% of the time
where the time goes in v3:
time: 108 us; the launch traced here: 107 us
  Pallas kernels  105 us (97%)
  matrix products  2.13 us (2%)
    pallas_call x1, Pallas kernels, shards(): pl.pallas_call(functools.partial(kernel, n_row, n_col, chunks, pairs_tota...  105 us

profile of v3, /device:TPU:0, one launch (start us, length us, event | category | flops | bytes accessed | tf_op | source)
XLA Modules:
  0.0 107.3 jit_solution(15325543095110284703)
XLA Ops:
  0.0 0.0 copy-start
  0.7 104.5 %gcn.1 = bf16[1024,256]{1,0:T(8,128)(2,1)} custom-call(s32[1,1]{1,0:T(1,128)S(6)} %copy.8.filled, s32[1,256]{1,0:T(1,128)} %bitcast.6, s32[1,256]{1,0:T(1,128)} %bitcast.7, bf16[1024,256]{1,0:T(8,128)(2,1)} %feat.1, bf16[256,256]{1,0:T(8,128)(2,1)} %w1.1, bf16[256,128,128]{2,1,0:T(8,128)(2,1)} %bitcast.5), custom_call_target="tpu_custom_call" | custom-call | tf_op jit(solution)/shard_map/gcn/pallas_call | solution.py:389
  105.2 0.0 copy-done
  105.2 2.1 %fusion = bf16[1024,256]{1,0:T(8,128)(2,1)} fusion(bf16[1024,256]{1,0:T(8,128)(2,1)} %gcn.1, bf16[256,256]{1,0:T(8,128)(2,1)S(1)} %copy-done), kind=kOutput, calls=%fused_computation.1 | convolution fusion | flops 134742016 | bytes 1179648 | tf_op jit(solution)/shard_map/dot_general | solution.py:419
Async XLA Ops:
  0.0 105.2 %copy-start = (bf16[256,256]{1,0:T(8,128)(2,1)S(1)}, bf16[256,256]{1,0:T(8,128)(2,1)}, u32[]{:S(2)}) copy-start(bf16[256,256]{1,0:T(8,128)(2,1)} %param.13) | copy-start | bytes 393220
